TPU v7x, 32 devices: a whole 2x2x4 slice. The times are simulated.
32 devices in a mesh: emit: 2 (over y), client: 16 (over z, x, core).
Axes of the slice: x: 2, y: 2, z: 4, core: 2. Of those that a mesh axis runs over, the one named last changes fastest.
Arguments:
- features: bfloat16 [65536, 768], P('client'), may hold values from -28 to 28
- labels: int32 [65536], P('client'), may hold values from 0 to 999
- client_ids: int32 [128], replicated, may hold values from 0 to 127, each once
- trunk_in: bfloat16 [128, 2048], replicated, may hold values from -6 to 6
- trunk_weight: bfloat16 [2048, 2048], P(None, 'client'), may hold values from -0.125 to 0.125
- class_table: bfloat16 [1000, 2048], P('emit'), may hold values from -6 to 6
- emit_weight: bfloat16 [2048, 768], P('emit'), may hold values from -0.125 to 0.125
Outputs:
- loss: float32 [65536], P('client')
- emit_grad: float32 [2048, 768], P(('emit', 'client'))
- trunk_grad: float32 [2048, 2048], P(None, ('emit', 'client'))
Inputs may be any that keep to these rules, and one draw needn't show every extreme that they name: Each client number appears once; slot s holds the features of client client_ids[s].
All inputs are finite; a program needn't handle non-finite values.
Results may differ from a plain program's by a relative error of at most 0.022.
Values may be sent and summed in bfloat16 or wider, within the bound.
No kernel may reach another device: no remote copies, remote signals or barrier semaphores. Data moves between devices by JAX's collectives and lax.ppermute only.
A program may use at most 128 MiB of HBM per device.

v0:
```python
import jax
import jax.numpy as jnp
from jax import lax
from jax.sharding import PartitionSpec as P

CL_DEV = 8


def silu_grad(value):
    sig = jax.nn.sigmoid(value)
    return sig * (1.0 + value * (1.0 - sig))


def per_device(features, labels, client_ids, trunk_in, trunk_weight, class_table, emit_weight):
    slots = CL_DEV
    clients = trunk_in.shape[0]
    hidden_dim = trunk_in.shape[1]
    classes = class_table.shape[0]
    feat_dim = features.shape[1]
    samples = features.shape[0] // slots
    client_index = lax.axis_index("client")
    emit_index = lax.axis_index("emit")
    pre_cols = jnp.dot(trunk_in, trunk_weight, preferred_element_type=jnp.float32).astype(
        jnp.bfloat16
    )
    pre_all = lax.all_gather(pre_cols, "client", axis=1, tiled=True)
    own_ids = lax.dynamic_slice_in_dim(client_ids, client_index * slots, slots)
    numbers = lax.iota(jnp.int32, clients)
    picker = (own_ids[:, None] == numbers[None, :]).astype(jnp.bfloat16)
    pre_own = jnp.dot(picker, pre_all, preferred_element_type=jnp.float32)
    code_in = jax.nn.silu(pre_own)[:, None, :] + class_table.astype(jnp.float32)[None, :, :]
    code = jax.nn.silu(code_in).astype(jnp.bfloat16).reshape(slots * classes, hidden_dim)
    emit_full = lax.all_gather(emit_weight, "emit", axis=0, tiled=True)
    heads = jnp.dot(code, emit_full, preferred_element_type=jnp.float32).astype(jnp.bfloat16)
    heads = heads.reshape(slots, classes, feat_dim)
    feats = features.reshape(slots, samples, feat_dim)
    logits = jnp.einsum("snd,skd->snk", feats, heads, preferred_element_type=jnp.float32)
    class_ids = emit_index * classes + lax.iota(jnp.int32, classes)
    onehot = (labels.reshape(slots, samples)[:, :, None] == class_ids[None, None, :]).astype(
        jnp.float32
    )
    target = jnp.sum(logits * onehot, axis=2)
    local_top = jnp.max(logits, axis=2)
    top = lax.pmax(local_top, "emit")
    expd = jnp.exp(logits - top[:, :, None])
    total, target_all = (
        lax.psum(jnp.sum(expd, axis=2).astype(jnp.bfloat16), "emit").astype(jnp.float32),
        lax.psum(target.astype(jnp.bfloat16), "emit").astype(jnp.float32),
    )
    loss = (top + jnp.log(total) - target_all).reshape(slots * samples)
    grad_logits = ((expd / total[:, :, None] - onehot) / clients).astype(jnp.bfloat16)
    grad_heads = jnp.einsum("snk,snd->skd", grad_logits, feats, preferred_element_type=jnp.float32)
    grad_heads = grad_heads.astype(jnp.bfloat16).reshape(slots * classes, feat_dim)
    partial_rows = lax.psum_scatter(
        jnp.einsum("rh,rd->hd", code, grad_heads, preferred_element_type=jnp.float32).astype(
            jnp.bfloat16
        ),
        "emit",
        scatter_dimension=0,
        tiled=True,
    )
    emit_grad = lax.psum_scatter(partial_rows, "client", scatter_dimension=0, tiled=True).astype(
        jnp.float32
    )
    grad_code = jnp.dot(grad_heads, emit_full.T, preferred_element_type=jnp.float32)
    grad_code = grad_code.reshape(slots, classes, hidden_dim)
    grad_sum = jnp.sum(grad_code * silu_grad(code_in), axis=1)
    block = hidden_dim // lax.axis_size("emit")
    grad_block = lax.psum_scatter(
        grad_sum.astype(jnp.bfloat16), "emit", scatter_dimension=1, tiled=True
    ).astype(jnp.float32)
    pre_block = lax.dynamic_slice_in_dim(pre_own, emit_index * block, block, 1)
    grad_pre = (grad_block * silu_grad(pre_block)).astype(jnp.bfloat16)
    grad_all = lax.all_gather(grad_pre, "client", axis=0, tiled=True)
    width = block // lax.axis_size("client")
    grad_mine = lax.dynamic_slice_in_dim(grad_all, client_index * width, width, 1)
    picker_all = (client_ids[:, None] == numbers[None, :]).astype(jnp.bfloat16)
    grad_client = jnp.einsum(
        "sc,sw->cw", picker_all, grad_mine, preferred_element_type=jnp.float32
    ).astype(jnp.bfloat16)
    trunk_grad = jnp.einsum("ch,cw->hw", trunk_in, grad_client, preferred_element_type=jnp.float32)
    return (loss, emit_grad, trunk_grad)


def solution(mesh):
    return jax.shard_map(
        per_device,
        mesh=mesh,
        in_specs=(
            P("client", None),
            P("client"),
            P(),
            P(),
            P(None, "client"),
            P("emit", None),
            P("emit", None),
        ),
        out_specs=(P("client"), P(("emit", "client"), None), P(None, ("emit", "client"))),
        check_vma=False,
    )
```

profile of v0, /device:TPU:0, one launch (start us, length us, event | category | flops | bytes accessed | tf_op | source)
XLA Modules:
  0.0 301.0 jit_solution(15818444923644420480)
XLA Ops:
  7.2 0.0 copy-start
  7.2 0.0 all-gather.2.cloned.1.call-start
  7.2 0.7 all-gather.2.cloned.1.call-update
  7.9 0.0 reduce-scatter.4.cloned.1.call-start
  8.0 4.1 %convert_element_type.57 = f32[500,2048]{1,0:T(8,128)} convert(bf16[500,2048]{1,0:T(8,128)(2,1)} %param.12) | non-fusion elementwise | flops 1024000 | bytes 6144000 | tf_op jit(solution)/shard_map/convert_element_type | solution.py:31
  12.1 0.7 dynamic_slice.9
  12.8 0.0 copy-done
  12.8 1.3 convolution_convert_fusion.1
  14.1 24.6 %all_gather.9 = bf16[128,2048]{1,0:T(8,128)(2,1)S(1)} all-gather(bf16[128,128]{1,0:T(8,128)(2,1)S(1)} %convolution_convert_fusion.1), channel_id=1, replica_groups=mesh['emit'=2,'client'=16] {'client'}, dimensions={1}, use_global_device_ids=true | all-gather | bytes 557056 | tf_op jit(solution)/shard_map/all_gather | solution.py:26
  38.7 0.9 divide_multiply_fusion
  39.6 12.5 %broadcast_add_fusion = f32[8,500,2048]{2,1,0:T(8,128)} fusion(f32[500,2048]{1,0:T(8,128)} %convert_element_type.57, f32[8,2048]{1,0:T(8,128)S(1)} %get-tuple-element.7), kind=kLoop, calls=%fused_computation.15 | loop fusion | flops 8192000 | bytes 36929536 | tf_op jit(solution)/shard_map/add | solution.py:31
  52.1 0.0 copy-start.3
  52.1 29.4 %add.75 = f32[4000,2048]{1,0:T(8,128)} reshape(f32[8,500,2048]{2,1,0:T(8,128)} %broadcast_add_fusion) | data formatting | bytes 65536000 | tf_op jit(solution)/shard_map/add | solution.py:31
  81.5 0.0 copy-done.3
  81.5 0.0 all-gather.2.cloned.1.call-done
  81.5 25.7 %fusion.20 = bf16[4000,768]{1,0:T(8,128)(2,1)} fusion(bf16[2048,768]{1,0:T(8,128)(2,1)} %all-gather.2.cloned.1.call-done, f32[4000,2048]{1,0:T(8,128)} %add.75), kind=kOutput, calls=%fused_computation.28 | convolution fusion | flops 12626944000 | bytes 42057728 | tf_op jit(solution)/shard_map/dot_general | solution.py:34
  107.2 6.3 %reshape.34 = bf16[8,500,768]{2,1,0:T(8,128)(2,1)} reshape(bf16[4000,768]{1,0:T(8,128)(2,1)} %fusion.20) | data formatting | bytes 12288000 | tf_op jit(solution)/shard_map/reshape | solution.py:35
  113.5 11.2 %bitcast_reduce_fusion = (f32[8,512]{1,0:T(8,128)S(1)}, f32[8,500,512]{2,1,0:T(8,128)}) fusion(bf16[8,500,768]{2,1,0:T(8,128)(2,1)} %reshape.34, bf16[8,512,768]{2,1,0:T(8,128)(2,1)} %bitcast.35), kind=kOutput, calls=%fused_computation.25 | convolution fusion | flops 3147771904 | bytes 20643840 | tf_op jit(solution)/shard_map/snd,skd->snk/dot_general | solution.py:37
  124.7 8.2 %pmax.7 = f32[8,512]{1,0:T(8,128)S(1)} all-reduce(f32[8,512]{1,0:T(8,128)S(1)} %get-tuple-element.9), channel_id=1, replica_groups=mesh['emit'=2,'client'=16] {'emit'}, use_global_device_ids=true, to_apply=%region_1.2 | all-reduce | flops 4096 | bytes 32768 | tf_op jit(solution)/shard_map/pmax | solution.py:44
  132.8 4.5 %fusion.19 = (bf16[8,512]{1,0:T(8,128)(2,1)S(1)}, bf16[8,512]{1,0:T(8,128)(2,1)S(1)}) fusion(f32[8,500,512]{2,1,0:T(8,128)} %get-tuple-element.10, f32[8,512]{1,0:T(8,128)S(1)} %pmax.7, s32[500]{0:T(512)S(1)} %iota_add_fusion, s32[8,512]{1,0:T(8,128)S(1)} %eq.44), kind=kLoop, calls=%fused_computation.27 | loop fusion | flops 10231808 | bytes 8243152 | tf_op jit(solution)/shard_map/reduce_sum | solution.py:47
  137.4 7.1 %all-reduce = (bf16[8,512]{1,0:T(8,128)(2,1)S(1)}, bf16[8,512]{1,0:T(8,128)(2,1)S(1)}) all-reduce(bf16[8,512]{1,0:T(8,128)(2,1)S(1)} %get-tuple-element.4, bf16[8,512]{1,0:T(8,128)(2,1)S(1)} %get-tuple-element.3), channel_id=1, replica_groups=mesh['emit'=2,'client'=16] {'emit'}, use_global_device_ids=true, to_apply=%region_5.6 | all-reduce | flops 8192 | bytes 32768 | tf_op jit(solution)/shard_map/psum | solution.py:48
  144.5 0.0 copy-start.1
  144.5 11.5 %fusion.30 = bf16[8,500,768]{2,1,0:T(8,128)(2,1)} fusion(bf16[8,512,768]{2,1,0:T(8,128)(2,1)} %bitcast.36, f32[8,500,512]{2,1,0:T(8,128)} %get-tuple-element.10, f32[8,512]{1,0:T(8,128)S(1)} %convert_element_type.61, s32[8,512]{1,0:T(8,128)S(1)} %eq.44, f32[8,512]{1,0:T(8,128)S(1)} %pmax.7, s32[500]{0:T(512)S(1)} %iota_add_fusion), kind=kOutput, calls=%fused_computation.36 | convolution fusion | flops 3163136000 | bytes 20678608 | tf_op jit(solution)/shard_map/snk,snd->skd/dot_general | solution.py:52
  156.0 0.0 copy-done.1
  156.0 20.2 %bitcast_convert_fusion = bf16[2048,768]{1,0:T(8,128)(2,1)} fusion(bf16[8,500,768]{2,1,0:T(8,128)(2,1)} %fusion.30, f32[500,2048]{1,0:T(8,128)S(1)} %copy-done.1, f32[8,2048]{1,0:T(8,128)S(1)} %get-tuple-element.7), kind=kOutput, calls=%fused_computation.29 | convolution fusion | flops 12633636864 | bytes 13451264 | tf_op jit(solution)/shard_map/rh,rd->hd/dot_general | solution.py:55
  176.2 0.0 reduce-scatter.4.cloned.1.call-update
  176.2 0.0 copy-start.2
  176.2 0.0 copy-start.4
  176.2 0.0 reduce-scatter.8.cloned.1.call-start
  176.3 24.4 %fusion.7 = bf16[8,2048]{1,0:T(8,128)(2,1)} fusion(bf16[8,500,768]{2,1,0:T(8,128)(2,1)} %fusion.30, f32[500,2048]{1,0:T(8,128)} %convert_element_type.57, f32[8,2048]{1,0:T(8,128)S(1)} %get-tuple-element.7, bf16[2048,768]{1,0:T(8,128)(2,1)} %all-gather.2.cloned.1.call-done), kind=kOutput, calls=%fused_computation.10 | convolution fusion | flops 12664815616 | bytes 13484032 | tf_op jit(solution)/shard_map/dot_general | solution.py:65
  200.7 0.0 reduce-scatter.8.cloned.1.call-update
  200.7 0.0 reduce-scatter.6.cloned.1.call-start
  200.8 16.3 %reduce-scatter.4.cloned.1.call-done = bf16[1024,768]{1,0:T(8,128)(2,1)} async-done(((bf16[2048,768]{1,0:T(8,128)(2,1)}), bf16[1024,768]{1,0:T(8,128)(2,1)}) %reduce-scatter.4.cloned.1.call-update) | async-done | bytes 1572880 | tf_op jit(solution)/shard_map/reduce_scatter | solution.py:54
  217.1 0.0 reduce-scatter.6.cloned.1.call-update
  217.1 0.6 copy.10
  217.7 12.1 %reduce-scatter.8.cloned.1.call-done = bf16[8,1024]{1,0:T(8,128)(2,1)} async-done(((bf16[8,2048]{1,0:T(8,128)(2,1)}), bf16[8,1024]{1,0:T(8,128)(2,1)}) %reduce-scatter.8.cloned.1.call-update) | async-done | bytes 16400 | tf_op jit(solution)/shard_map/reduce_scatter | solution.py:69
  229.8 0.0 copy-done.2
  229.8 0.7 multiply_convert_fusion.4
  230.6 22.0 %all_gather.11 = bf16[128,1024]{1,0:T(8,128)(2,1)S(1)} all-gather(bf16[8,1024]{1,0:T(8,128)(2,1)S(1)} %multiply_convert_fusion.4), channel_id=1, replica_groups=mesh['emit'=2,'client'=16] {'client'}, dimensions={0}, use_global_device_ids=true | all-gather | bytes 278528 | tf_op jit(solution)/shard_map/all_gather | solution.py:74
  252.6 0.0 copy-done.4
  252.6 1.3 convolution_bitcast_fusion
  253.9 39.0 %reduce-scatter.6.cloned.1.call-done = bf16[64,768]{1,0:T(8,128)(2,1)} async-done(((bf16[1024,768]{1,0:T(8,128)(2,1)}), bf16[64,768]{1,0:T(8,128)(2,1)}) %reduce-scatter.6.cloned.1.call-update) | async-done | bytes 98320 | tf_op jit(solution)/shard_map/reduce_scatter | solution.py:62
  292.9 1.6 convert_element_type.69
  (4 shorter events, 0.0 us)
Async XLA Ops:
  7.2 5.6 %copy-start = (bf16[128,2048]{1,0:T(8,128)(2,1)S(1)}, bf16[128,2048]{1,0:T(8,128)(2,1)}, u32[]{:S(2)}) copy-start(bf16[128,2048]{1,0:T(8,128)(2,1)} %param.10) | copy-start | bytes 1572868
  7.2 74.3 %all-gather.2.cloned.1.call-start = ((), (), s32[]{:S(2)}) async-start(), calls=%async_computation.3 | async-start | bytes 4718592 | tf_op jit(solution)/shard_map/all_gather | solution.py:33
  7.9 209.2 %reduce-scatter.4.cloned.1.call-start = ((), (), s32[]{:S(2)}) async-start(), calls=%async_computation.4 | async-start | bytes 4718592 | tf_op jit(solution)/shard_map/reduce_scatter | solution.py:54
  52.1 29.4 %copy-start.3 = (s32[4096]{0:T(1024)S(1)}, s32[4096]{0:T(1024)}, u32[]{:S(2)}) copy-start(s32[4096]{0:T(1024)} %param.8) | copy-start | bytes 49156
  144.5 11.5 %copy-start.1 = (f32[500,2048]{1,0:T(8,128)S(1)}, f32[500,2048]{1,0:T(8,128)}, u32[]{:S(2)}) copy-start(f32[500,2048]{1,0:T(8,128)} %convert_element_type.57) | copy-start | bytes 12288004
  176.2 53.6 %copy-start.2 = (f32[8,2048]{1,0:T(8,128)S(1)}, f32[8,2048]{1,0:T(8,128)}, u32[]{:S(2)}) copy-start(f32[8,2048]{1,0:T(8,128)} %get-tuple-element.8) | copy-start | bytes 196612
  176.2 76.4 %copy-start.4 = (s32[128]{0:T(128)S(1)}, s32[128]{0:T(128)}, u32[]{:S(2)}) copy-start(s32[128]{0:T(128)} %param.9) | copy-start | bytes 1540
  176.2 53.6 %reduce-scatter.8.cloned.1.call-start = ((), (), s32[]{:S(2)}) async-start(), calls=%async_computation.6 | async-start | bytes 49152 | tf_op jit(solution)/shard_map/reduce_scatter | solution.py:69
  200.7 92.2 %reduce-scatter.6.cloned.1.call-start = ((), (), s32[]{:S(2)}) async-start(), calls=%async_computation.5 | async-start | bytes 1671168 | tf_op jit(solution)/shard_map/reduce_scatter | solution.py:62
Sparse Core Ops, SparseCore 0:
  9.5 47.6 all-gather.1
  176.3 40.7 reduce-scatter.3
  219.8 9.9 reduce-scatter.7
  233.3 59.5 reduce-scatter.5
where the time goes:
time: 302 us; the launch traced here: 301 us
  matrix products  96.5 us (32%)
  waiting for transfers between devices  68.1 us (23%)
  blocking collectives  61.9 us (20%)
  local copies, waits for them, and re-layouts  37.1 us (12%)
  other arithmetic  23.4 us (8%)
  between operations  13.8 us (5%)
    reduce_scatter x1, waiting for transfers between devices, per_device(): lax.psum_scatter(partial_rows, 'client', scatter_dimension=0, tiled=True)  39 us
    add x1, local copies, waits for them, and re-layouts, per_device(): jax.nn.silu(pre_own)[:, None, :]  29.4 us
    dot_general x1, matrix products, per_device(): jnp.dot(code, emit_full, preferred_element_type=jnp.float32)  25.7 us
    all_gather x1, blocking collectives, per_device(): pre_all = lax.all_gather(pre_cols, 'client', axis=1, tiled=True)  24.6 us
    dot_general x1, matrix products, per_device(): jnp.dot(grad_heads, emit_full.T, preferred_element_type=jnp.float32)  24.4 us
    all_gather x1, blocking collectives, per_device(): grad_all = lax.all_gather(grad_pre, 'client', axis=0, tiled=True)  22 us
    dot_general x1, matrix products, per_device(): jnp.einsum('rh,rd->hd', code, grad_heads, preferred_element_type=jnp.floa...  20.2 us
    reduce_scatter x1, waiting for transfers between devices, per_device(): lax.psum_scatter(jnp.einsum('rh,rd->hd', code, grad_heads, preferred_elem...  16.3 us
  transfers between devices with their start and end apart: 4, of which 3 were waited for; matrix products, arithmetic and copies ran while one was open for 25% of the time, Pallas kernels for 0%

commit v1 on v0

--- a/solution.py
+++ b/solution.py
@@ -71,7 +71,14 @@
     ).astype(jnp.float32)
     pre_block = lax.dynamic_slice_in_dim(pre_own, emit_index * block, block, 1)
     grad_pre = (grad_block * silu_grad(pre_block)).astype(jnp.bfloat16)
-    grad_all = lax.all_gather(grad_pre, "client", axis=0, tiled=True)
+    count = lax.axis_size("client")
+    hops = [(i, (i + 1) % count) for i in range(count)]
+    shards = [grad_pre]
+    for far in range(1, count):
+        shards = [lax.ppermute(shards[0], "client", hops), *shards]
+    whole = jnp.concatenate(shards, axis=0)
+    shift = (lax.axis_index("client") + 1) * shards[-1].shape[0]
+    grad_all = jnp.roll(whole, shift, axis=0)
     width = block // lax.axis_size("client")
     grad_mine = lax.dynamic_slice_in_dim(grad_all, client_index * width, width, 1)
     picker_all = (client_ids[:, None] == numbers[None, :]).astype(jnp.bfloat16)

time: 302 us -> 356 us (1.18)
  waiting for transfers between devices: 68.1 us -> 143 us
  blocking collectives: 61.9 us -> 39.9 us
    ppermute x0 -> x15, waiting for transfers between devices: none -> 87.2 us  [per_device(): shards = [lax.ppermute(shards[0], 'client', hops), *shards]]
    all_gather x1 -> x0, blocking collectives: 22 us -> none  [per_device(): grad_all = lax.all_gather(grad_pre, 'client', axis=0, tiled=True)]
    reduce_scatter x1, waiting for transfers between devices: 39 us -> 55.4 us  [per_device(): lax.psum_scatter(partial_rows, 'client', scatter_dimension=0, tiled=True)]
    reduce_scatter x1, waiting for transfers between devices: 16.3 us -> 0.02 us  [per_device(): lax.psum_scatter(jnp.einsum('rh,rd->hd', code, grad_heads, preferred_elem...]
    reduce_scatter x1, waiting for transfers between devices: 12.1 us -> 0.02 us  [per_device(): lax.psum_scatter(grad_sum.astype(jnp.bfloat16), 'emit', scatter_dimension...]
  transfers between devices with their start and end apart: 4 -> 19, of which waited for: 3 -> 16; matrix products, arithmetic and copies ran while one was open for 25% -> 20% of each run, Pallas kernels for 0% -> 0%
where the time goes in v1:
time: 356 us; the launch traced here: 355 us
  waiting for transfers between devices  143 us (40%)
  matrix products  97 us (27%)
  blocking collectives  39.9 us (11%)
  local copies, waits for them, and re-layouts  37.1 us (10%)
  other arithmetic  23.4 us (7%)
  between operations  14.1 us (4%)
    ppermute x15, waiting for transfers between devices, per_device(): shards = [lax.ppermute(shards[0], 'client', hops), *shards]  87.2 us
    reduce_scatter x1, waiting for transfers between devices, per_device(): lax.psum_scatter(partial_rows, 'client', scatter_dimension=0, tiled=True)  55.4 us
    add x1, local copies, waits for them, and re-layouts, per_device(): jax.nn.silu(pre_own)[:, None, :]  29.3 us
    dot_general x1, matrix products, per_device(): jnp.dot(code, emit_full, preferred_element_type=jnp.float32)  25.7 us
    dot_general x1, matrix products, per_device(): jnp.dot(grad_heads, emit_full.T, preferred_element_type=jnp.float32)  24.6 us
    all_gather x1, blocking collectives, per_device(): pre_all = lax.all_gather(pre_cols, 'client', axis=1, tiled=True)  24.6 us
    dot_general x1, matrix products, per_device(): jnp.einsum('rh,rd->hd', code, grad_heads, preferred_element_type=jnp.floa...  20.5 us
    add x1, other arithmetic, per_device(): jax.nn.silu(pre_own)[:, None, :]  12.5 us
  transfers between devices with their start and end apart: 19, of which 16 were waited for; matrix products, arithmetic and copies ran while one was open for 20% of the time, Pallas kernels for 0%

profile of v1, /device:TPU:0, one launch (start us, length us, event | category | flops | bytes accessed | tf_op | source)
XLA Modules:
  0.0 355.1 jit_solution(14560624058617870971)
XLA Ops:
  7.2 0.0 copy-start
  7.2 0.0 all-gather.2.cloned.1.call-start
  7.2 0.7 all-gather.2.cloned.1.call-update
  7.9 0.0 reduce-scatter.8.cloned.1.call-start
  8.0 4.1 %convert_element_type.57 = f32[500,2048]{1,0:T(8,128)} convert(bf16[500,2048]{1,0:T(8,128)(2,1)} %param.12) | non-fusion elementwise | flops 1024000 | bytes 6144000 | tf_op jit(solution)/shard_map/convert_element_type | solution.py:31
  12.0 0.7 dynamic_slice.11
  12.8 1.3 convolution_convert_fusion.1
  14.1 24.6 %all_gather.6 = bf16[128,2048]{1,0:T(8,128)(2,1)S(1)} all-gather(bf16[128,128]{1,0:T(8,128)(2,1)S(1)} %convolution_convert_fusion.1), channel_id=1, replica_groups=mesh['emit'=2,'client'=16] {'client'}, dimensions={1}, use_global_device_ids=true | all-gather | bytes 557056 | tf_op jit(solution)/shard_map/all_gather | solution.py:26
  38.7 0.9 divide_multiply_fusion
  39.6 12.5 %broadcast_add_fusion = f32[8,500,2048]{2,1,0:T(8,128)} fusion(f32[500,2048]{1,0:T(8,128)} %convert_element_type.57, f32[8,2048]{1,0:T(8,128)S(1)} %get-tuple-element.7), kind=kLoop, calls=%fused_computation.15 | loop fusion | flops 8192000 | bytes 36929536 | tf_op jit(solution)/shard_map/add | solution.py:31
  52.0 29.3 %add.90 = f32[4000,2048]{1,0:T(8,128)} reshape(f32[8,500,2048]{2,1,0:T(8,128)} %broadcast_add_fusion) | data formatting | bytes 65536000 | tf_op jit(solution)/shard_map/add | solution.py:31
  81.4 0.0 all-gather.2.cloned.1.call-done
  81.4 25.7 %fusion.20 = bf16[4000,768]{1,0:T(8,128)(2,1)} fusion(bf16[2048,768]{1,0:T(8,128)(2,1)} %all-gather.2.cloned.1.call-done, f32[4000,2048]{1,0:T(8,128)} %add.90), kind=kOutput, calls=%fused_computation.28 | convolution fusion | flops 12626944000 | bytes 42057728 | tf_op jit(solution)/shard_map/dot_general | solution.py:34
  107.1 6.3 %reshape.34 = bf16[8,500,768]{2,1,0:T(8,128)(2,1)} reshape(bf16[4000,768]{1,0:T(8,128)(2,1)} %fusion.20) | data formatting | bytes 12288000 | tf_op jit(solution)/shard_map/reshape | solution.py:35
  113.4 11.2 %bitcast_reduce_fusion = (f32[8,512]{1,0:T(8,128)S(1)}, f32[8,500,512]{2,1,0:T(8,128)}) fusion(bf16[8,500,768]{2,1,0:T(8,128)(2,1)} %reshape.34, bf16[8,512,768]{2,1,0:T(8,128)(2,1)} %bitcast.35), kind=kOutput, calls=%fused_computation.25 | convolution fusion | flops 3147771904 | bytes 20643840 | tf_op jit(solution)/shard_map/snd,skd->snk/dot_general | solution.py:37
  124.5 8.2 %pmax.7 = f32[8,512]{1,0:T(8,128)S(1)} all-reduce(f32[8,512]{1,0:T(8,128)S(1)} %get-tuple-element.9), channel_id=1, replica_groups=mesh['emit'=2,'client'=16] {'emit'}, use_global_device_ids=true, to_apply=%region_1.2 | all-reduce | flops 4096 | bytes 32768 | tf_op jit(solution)/shard_map/pmax | solution.py:44
  132.7 4.5 %fusion.19 = (bf16[8,512]{1,0:T(8,128)(2,1)S(1)}, bf16[8,512]{1,0:T(8,128)(2,1)S(1)}) fusion(f32[8,500,512]{2,1,0:T(8,128)} %get-tuple-element.10, f32[8,512]{1,0:T(8,128)S(1)} %pmax.7, s32[500]{0:T(512)S(1)} %iota_add_fusion, s32[8,512]{1,0:T(8,128)S(1)} %eq.47), kind=kLoop, calls=%fused_computation.27 | loop fusion | flops 10231808 | bytes 8243152 | tf_op jit(solution)/shard_map/reduce_sum | solution.py:47
  137.3 7.1 %all-reduce = (bf16[8,512]{1,0:T(8,128)(2,1)S(1)}, bf16[8,512]{1,0:T(8,128)(2,1)S(1)}) all-reduce(bf16[8,512]{1,0:T(8,128)(2,1)S(1)} %get-tuple-element.4, bf16[8,512]{1,0:T(8,128)(2,1)S(1)} %get-tuple-element.3), channel_id=1, replica_groups=mesh['emit'=2,'client'=16] {'emit'}, use_global_device_ids=true, to_apply=%region_5.6 | all-reduce | flops 8192 | bytes 32768 | tf_op jit(solution)/shard_map/psum | solution.py:48
  144.4 11.5 %fusion.30 = bf16[8,500,768]{2,1,0:T(8,128)(2,1)} fusion(bf16[8,512,768]{2,1,0:T(8,128)(2,1)} %bitcast.36, f32[8,500,512]{2,1,0:T(8,128)} %get-tuple-element.10, f32[8,512]{1,0:T(8,128)S(1)} %convert_element_type.61, s32[8,512]{1,0:T(8,128)S(1)} %eq.47, f32[8,512]{1,0:T(8,128)S(1)} %pmax.7, s32[500]{0:T(512)S(1)} %iota_add_fusion), kind=kOutput, calls=%fused_computation.36 | convolution fusion | flops 3163136000 | bytes 20678608 | tf_op jit(solution)/shard_map/snk,snd->skd/dot_general | solution.py:52
  155.8 24.6 %fusion.7 = bf16[8,2048]{1,0:T(8,128)(2,1)} fusion(bf16[8,500,768]{2,1,0:T(8,128)(2,1)} %fusion.30, f32[500,2048]{1,0:T(8,128)S(1)} %copy-done.1, f32[8,2048]{1,0:T(8,128)S(1)} %get-tuple-element.7, bf16[2048,768]{1,0:T(8,128)(2,1)} %all-gather.2.cloned.1.call-done), kind=kOutput, calls=%fused_computation.10 | convolution fusion | flops 12664815616 | bytes 13484032 | tf_op jit(solution)/shard_map/dot_general | solution.py:65
  180.4 0.0 reduce-scatter.8.cloned.1.call-update
  180.5 0.0 copy-start.2
  180.5 0.0 copy-start.4
  180.5 0.0 reduce-scatter.4.cloned.1.call-start
  180.5 20.5 %bitcast_convert_fusion = bf16[2048,768]{1,0:T(8,128)(2,1)} fusion(bf16[8,500,768]{2,1,0:T(8,128)(2,1)} %fusion.30, f32[500,2048]{1,0:T(8,128)} %convert_element_type.57, f32[8,2048]{1,0:T(8,128)S(1)} %get-tuple-element.7), kind=kOutput, calls=%fused_computation.29 | convolution fusion | flops 12633636864 | bytes 13451264 | tf_op jit(solution)/shard_map/rh,rd->hd/dot_general | solution.py:55
  201.1 0.0 reduce-scatter.4.cloned.1.call-update
  201.1 0.0 reduce-scatter.6.cloned.1.call-start
  201.1 0.0 reduce-scatter.8.cloned.1.call-done
  201.2 0.7 multiply_convert_fusion.4
  201.9 0.1 collective-permute-start
  202.0 5.8 %collective-permute-done = bf16[8,1024]{1,0:T(8,128)(2,1)S(1)} collective-permute-done((bf16[8,1024]{1,0:T(8,128)(2,1)S(1)}, bf16[8,1024]{1,0:T(8,128)(2,1)S(1)}, u32[]{:S(2)}, u32[]{:S(2)}) %collective-permute-start) | collective-permute-done | bytes 16416 | tf_op jit(solution)/shard_map/ppermute | solution.py:78
  207.8 0.0 collective-permute-start.1
  207.8 5.9 %collective-permute-done.1 = bf16[8,1024]{1,0:T(8,128)(2,1)S(1)} collective-permute-done((bf16[8,1024]{1,0:T(8,128)(2,1)S(1)}, bf16[8,1024]{1,0:T(8,128)(2,1)S(1)}, u32[]{:S(2)}, u32[]{:S(2)}) %collective-permute-start.1) | collective-permute-done | bytes 16416 | tf_op jit(solution)/shard_map/ppermute | solution.py:78
  213.7 0.0 collective-permute-start.2
  213.7 5.9 %collective-permute-done.2 = bf16[8,1024]{1,0:T(8,128)(2,1)S(1)} collective-permute-done((bf16[8,1024]{1,0:T(8,128)(2,1)S(1)}, bf16[8,1024]{1,0:T(8,128)(2,1)S(1)}, u32[]{:S(2)}, u32[]{:S(2)}) %collective-permute-start.2) | collective-permute-done | bytes 16416 | tf_op jit(solution)/shard_map/ppermute | solution.py:78
  219.6 0.0 collective-permute-start.3
  219.6 5.9 %collective-permute-done.3 = bf16[8,1024]{1,0:T(8,128)(2,1)S(1)} collective-permute-done((bf16[8,1024]{1,0:T(8,128)(2,1)S(1)}, bf16[8,1024]{1,0:T(8,128)(2,1)S(1)}, u32[]{:S(2)}, u32[]{:S(2)}) %collective-permute-start.3) | collective-permute-done | bytes 16416 | tf_op jit(solution)/shard_map/ppermute | solution.py:78
  225.4 0.0 collective-permute-start.4
  225.4 5.9 %collective-permute-done.4 = bf16[8,1024]{1,0:T(8,128)(2,1)S(1)} collective-permute-done((bf16[8,1024]{1,0:T(8,128)(2,1)S(1)}, bf16[8,1024]{1,0:T(8,128)(2,1)S(1)}, u32[]{:S(2)}, u32[]{:S(2)}) %collective-permute-start.4) | collective-permute-done | bytes 16416 | tf_op jit(solution)/shard_map/ppermute | solution.py:78
  231.3 0.0 collective-permute-start.5
  231.3 5.9 %collective-permute-done.5 = bf16[8,1024]{1,0:T(8,128)(2,1)S(1)} collective-permute-done((bf16[8,1024]{1,0:T(8,128)(2,1)S(1)}, bf16[8,1024]{1,0:T(8,128)(2,1)S(1)}, u32[]{:S(2)}, u32[]{:S(2)}) %collective-permute-start.5) | collective-permute-done | bytes 16416 | tf_op jit(solution)/shard_map/ppermute | solution.py:78
  237.1 0.0 collective-permute-start.6
  237.1 5.9 %collective-permute-done.6 = bf16[8,1024]{1,0:T(8,128)(2,1)S(1)} collective-permute-done((bf16[8,1024]{1,0:T(8,128)(2,1)S(1)}, bf16[8,1024]{1,0:T(8,128)(2,1)S(1)}, u32[]{:S(2)}, u32[]{:S(2)}) %collective-permute-start.6) | collective-permute-done | bytes 16416 | tf_op jit(solution)/shard_map/ppermute | solution.py:78
  243.0 0.0 collective-permute-start.7
  243.0 5.9 %collective-permute-done.7 = bf16[8,1024]{1,0:T(8,128)(2,1)S(1)} collective-permute-done((bf16[8,1024]{1,0:T(8,128)(2,1)S(1)}, bf16[8,1024]{1,0:T(8,128)(2,1)S(1)}, u32[]{:S(2)}, u32[]{:S(2)}) %collective-permute-start.7) | collective-permute-done | bytes 16416 | tf_op jit(solution)/shard_map/ppermute | solution.py:78
  248.9 0.0 collective-permute-start.8
  248.9 5.9 %collective-permute-done.8 = bf16[8,1024]{1,0:T(8,128)(2,1)S(1)} collective-permute-done((bf16[8,1024]{1,0:T(8,128)(2,1)S(1)}, bf16[8,1024]{1,0:T(8,128)(2,1)S(1)}, u32[]{:S(2)}, u32[]{:S(2)}) %collective-permute-start.8) | collective-permute-done | bytes 16416 | tf_op jit(solution)/shard_map/ppermute | solution.py:78
  254.7 0.0 collective-permute-start.9
  254.7 5.9 %collective-permute-done.9 = bf16[8,1024]{1,0:T(8,128)(2,1)S(1)} collective-permute-done((bf16[8,1024]{1,0:T(8,128)(2,1)S(1)}, bf16[8,1024]{1,0:T(8,128)(2,1)S(1)}, u32[]{:S(2)}, u32[]{:S(2)}) %collective-permute-start.9) | collective-permute-done | bytes 16416 | tf_op jit(solution)/shard_map/ppermute | solution.py:78
  260.6 0.0 collective-permute-start.10
  260.6 5.9 %collective-permute-done.10 = bf16[8,1024]{1,0:T(8,128)(2,1)S(1)} collective-permute-done((bf16[8,1024]{1,0:T(8,128)(2,1)S(1)}, bf16[8,1024]{1,0:T(8,128)(2,1)S(1)}, u32[]{:S(2)}, u32[]{:S(2)}) %collective-permute-start.10) | collective-permute-done | bytes 16416 | tf_op jit(solution)/shard_map/ppermute | solution.py:78
  266.5 0.0 collective-permute-start.11
  266.5 5.9 %collective-permute-done.11 = bf16[8,1024]{1,0:T(8,128)(2,1)S(1)} collective-permute-done((bf16[8,1024]{1,0:T(8,128)(2,1)S(1)}, bf16[8,1024]{1,0:T(8,128)(2,1)S(1)}, u32[]{:S(2)}, u32[]{:S(2)}) %collective-permute-start.11) | collective-permute-done | bytes 16416 | tf_op jit(solution)/shard_map/ppermute | solution.py:78
  272.3 0.0 collective-permute-start.12
  272.3 5.9 %collective-permute-done.12 = bf16[8,1024]{1,0:T(8,128)(2,1)S(1)} collective-permute-done((bf16[8,1024]{1,0:T(8,128)(2,1)S(1)}, bf16[8,1024]{1,0:T(8,128)(2,1)S(1)}, u32[]{:S(2)}, u32[]{:S(2)}) %collective-permute-start.12) | collective-permute-done | bytes 16416 | tf_op jit(solution)/shard_map/ppermute | solution.py:78
  278.2 5.9 %collective-permute-done.13 = bf16[8,1024]{1,0:T(8,128)(2,1)S(1)} collective-permute-done((bf16[8,1024]{1,0:T(8,128)(2,1)S(1)}, bf16[8,1024]{1,0:T(8,128)(2,1)S(1)}, u32[]{:S(2)}, u32[]{:S(2)}) %collective-permute-start.13) | collective-permute-done | bytes 16416 | tf_op jit(solution)/shard_map/ppermute | solution.py:78
  284.0 0.0 collective-permute-start.14
  284.1 0.6 copy.10
  284.7 5.2 %collective-permute-done.14 = bf16[8,1024]{1,0:T(8,128)(2,1)S(1)} collective-permute-done((bf16[8,1024]{1,0:T(8,128)(2,1)S(1)}, bf16[8,1024]{1,0:T(8,128)(2,1)S(1)}, u32[]{:S(2)}, u32[]{:S(2)}) %collective-permute-start.14) | collective-permute-done | bytes 16416 | tf_op jit(solution)/shard_map/ppermute | solution.py:78
  290.0 0.0 reduce-scatter.4.cloned.1.call-done
  290.1 0.0 reduce-scatter.6.cloned.1.call-update
  290.3 1.3 convolution_bitcast_fusion
  291.6 55.4 %reduce-scatter.6.cloned.1.call-done = bf16[64,768]{1,0:T(8,128)(2,1)} async-done(((bf16[1024,768]{1,0:T(8,128)(2,1)}), bf16[64,768]{1,0:T(8,128)(2,1)}) %reduce-scatter.6.cloned.1.call-update) | async-done | bytes 98320 | tf_op jit(solution)/shard_map/reduce_scatter | solution.py:62
  347.0 1.6 convert_element_type.69
  (44 shorter events, 0.2 us)
Async XLA Ops:
  7.2 5.6 %copy-start = (bf16[128,2048]{1,0:T(8,128)(2,1)S(1)}, bf16[128,2048]{1,0:T(8,128)(2,1)}, u32[]{:S(2)}) copy-start(bf16[128,2048]{1,0:T(8,128)(2,1)} %param.10) | copy-start | bytes 1572868
  7.2 74.2 %all-gather.2.cloned.1.call-start = ((), (), s32[]{:S(2)}) async-start(), calls=%async_computation.3 | async-start | bytes 4718592 | tf_op jit(solution)/shard_map/all_gather | solution.py:33
  7.9 193.2 %reduce-scatter.8.cloned.1.call-start = ((), (), s32[]{:S(2)}) async-start(), calls=%async_computation.6 | async-start | bytes 49152 | tf_op jit(solution)/shard_map/reduce_scatter | solution.py:69
  52.0 29.3 %copy-start.3 = (s32[4096]{0:T(1024)S(1)}, s32[4096]{0:T(1024)}, u32[]{:S(2)}) copy-start(s32[4096]{0:T(1024)} %param.8) | copy-start | bytes 49156
  144.4 11.5 %copy-start.1 = (f32[500,2048]{1,0:T(8,128)S(1)}, f32[500,2048]{1,0:T(8,128)}, u32[]{:S(2)}) copy-start(f32[500,2048]{1,0:T(8,128)} %convert_element_type.57) | copy-start | bytes 12288004
  180.5 20.7 %copy-start.2 = (f32[8,2048]{1,0:T(8,128)S(1)}, f32[8,2048]{1,0:T(8,128)}, u32[]{:S(2)}) copy-start(f32[8,2048]{1,0:T(8,128)} %get-tuple-element.8) | copy-start | bytes 196612
  180.5 109.8 %copy-start.4 = (s32[128]{0:T(128)S(1)}, s32[128]{0:T(128)}, u32[]{:S(2)}) copy-start(s32[128]{0:T(128)} %param.9) | copy-start | bytes 1540
  180.5 109.6 %reduce-scatter.4.cloned.1.call-start = ((), (), s32[]{:S(2)}) async-start(), calls=%async_computation.4 | async-start | bytes 4718592 | tf_op jit(solution)/shard_map/reduce_scatter | solution.py:54
  201.1 145.9 %reduce-scatter.6.cloned.1.call-start = ((), (), s32[]{:S(2)}) async-start(), calls=%async_computation.5 | async-start | bytes 1671168 | tf_op jit(solution)/shard_map/reduce_scatter | solution.py:62
  201.9 5.9 %collective-permute-start = (bf16[8,1024]{1,0:T(8,128)(2,1)S(1)}, bf16[8,1024]{1,0:T(8,128)(2,1)S(1)}, u32[]{:S(2)}, u32[]{:S(2)}) collective-permute-start(bf16[8,1024]{1,0:T(8,128)(2,1)S(1)} %multiply_convert_fusion.4), channel_id=1, source_target_pairs={{0,1},{1,2},{2,3},{3,4},{4,5},{5,6},{6,7},{7,8},{8,9},{9,10},{10,1... | collective-permute-start | bytes 49160 | tf_op jit(solution)/shard_map/ppermute | solution.py:78
  207.8 5.9 %collective-permute-start.1 = (bf16[8,1024]{1,0:T(8,128)(2,1)S(1)}, bf16[8,1024]{1,0:T(8,128)(2,1)S(1)}, u32[]{:S(2)}, u32[]{:S(2)}) collective-permute-start(bf16[8,1024]{1,0:T(8,128)(2,1)S(1)} %collective-permute-done), channel_id=1, source_target_pairs={{0,1},{1,2},{2,3},{3,4},{4,5},{5,6},{6,7},{7,8},{8,9},{9,10},{10,1... | collective-permute-start | bytes 49160 | tf_op jit(solution)/shard_map/ppermute | solution.py:78
  213.7 5.9 %collective-permute-start.2 = (bf16[8,1024]{1,0:T(8,128)(2,1)S(1)}, bf16[8,1024]{1,0:T(8,128)(2,1)S(1)}, u32[]{:S(2)}, u32[]{:S(2)}) collective-permute-start(bf16[8,1024]{1,0:T(8,128)(2,1)S(1)} %collective-permute-done.1), channel_id=1, source_target_pairs={{0,1},{1,2},{2,3},{3,4},{4,5},{5,6},{6,7},{7,8},{8,9},{9,10},{10,1... | collective-permute-start | bytes 49160 | tf_op jit(solution)/shard_map/ppermute | solution.py:78
  219.6 5.9 %collective-permute-start.3 = (bf16[8,1024]{1,0:T(8,128)(2,1)S(1)}, bf16[8,1024]{1,0:T(8,128)(2,1)S(1)}, u32[]{:S(2)}, u32[]{:S(2)}) collective-permute-start(bf16[8,1024]{1,0:T(8,128)(2,1)S(1)} %collective-permute-done.2), channel_id=1, source_target_pairs={{0,1},{1,2},{2,3},{3,4},{4,5},{5,6},{6,7},{7,8},{8,9},{9,10},{10,1... | collective-permute-start | bytes 49160 | tf_op jit(solution)/shard_map/ppermute | solution.py:78
  225.4 5.9 %collective-permute-start.4 = (bf16[8,1024]{1,0:T(8,128)(2,1)S(1)}, bf16[8,1024]{1,0:T(8,128)(2,1)S(1)}, u32[]{:S(2)}, u32[]{:S(2)}) collective-permute-start(bf16[8,1024]{1,0:T(8,128)(2,1)S(1)} %collective-permute-done.3), channel_id=1, source_target_pairs={{0,1},{1,2},{2,3},{3,4},{4,5},{5,6},{6,7},{7,8},{8,9},{9,10},{10,1... | collective-permute-start | bytes 49160 | tf_op jit(solution)/shard_map/ppermute | solution.py:78
  231.3 5.9 %collective-permute-start.5 = (bf16[8,1024]{1,0:T(8,128)(2,1)S(1)}, bf16[8,1024]{1,0:T(8,128)(2,1)S(1)}, u32[]{:S(2)}, u32[]{:S(2)}) collective-permute-start(bf16[8,1024]{1,0:T(8,128)(2,1)S(1)} %collective-permute-done.4), channel_id=1, source_target_pairs={{0,1},{1,2},{2,3},{3,4},{4,5},{5,6},{6,7},{7,8},{8,9},{9,10},{10,1... | collective-permute-start | bytes 49160 | tf_op jit(solution)/shard_map/ppermute | solution.py:78
  237.1 5.9 %collective-permute-start.6 = (bf16[8,1024]{1,0:T(8,128)(2,1)S(1)}, bf16[8,1024]{1,0:T(8,128)(2,1)S(1)}, u32[]{:S(2)}, u32[]{:S(2)}) collective-permute-start(bf16[8,1024]{1,0:T(8,128)(2,1)S(1)} %collective-permute-done.5), channel_id=1, source_target_pairs={{0,1},{1,2},{2,3},{3,4},{4,5},{5,6},{6,7},{7,8},{8,9},{9,10},{10,1... | collective-permute-start | bytes 49160 | tf_op jit(solution)/shard_map/ppermute | solution.py:78
  243.0 5.9 %collective-permute-start.7 = (bf16[8,1024]{1,0:T(8,128)(2,1)S(1)}, bf16[8,1024]{1,0:T(8,128)(2,1)S(1)}, u32[]{:S(2)}, u32[]{:S(2)}) collective-permute-start(bf16[8,1024]{1,0:T(8,128)(2,1)S(1)} %collective-permute-done.6), channel_id=1, source_target_pairs={{0,1},{1,2},{2,3},{3,4},{4,5},{5,6},{6,7},{7,8},{8,9},{9,10},{10,1... | collective-permute-start | bytes 49160 | tf_op jit(solution)/shard_map/ppermute | solution.py:78
  248.9 5.9 %collective-permute-start.8 = (bf16[8,1024]{1,0:T(8,128)(2,1)S(1)}, bf16[8,1024]{1,0:T(8,128)(2,1)S(1)}, u32[]{:S(2)}, u32[]{:S(2)}) collective-permute-start(bf16[8,1024]{1,0:T(8,128)(2,1)S(1)} %collective-permute-done.7), channel_id=1, source_target_pairs={{0,1},{1,2},{2,3},{3,4},{4,5},{5,6},{6,7},{7,8},{8,9},{9,10},{10,1... | collective-permute-start | bytes 49160 | tf_op jit(solution)/shard_map/ppermute | solution.py:78
  254.7 5.9 %collective-permute-start.9 = (bf16[8,1024]{1,0:T(8,128)(2,1)S(1)}, bf16[8,1024]{1,0:T(8,128)(2,1)S(1)}, u32[]{:S(2)}, u32[]{:S(2)}) collective-permute-start(bf16[8,1024]{1,0:T(8,128)(2,1)S(1)} %collective-permute-done.8), channel_id=1, source_target_pairs={{0,1},{1,2},{2,3},{3,4},{4,5},{5,6},{6,7},{7,8},{8,9},{9,10},{10,1... | collective-permute-start | bytes 49160 | tf_op jit(solution)/shard_map/ppermute | solution.py:78
  260.6 5.9 %collective-permute-start.10 = (bf16[8,1024]{1,0:T(8,128)(2,1)S(1)}, bf16[8,1024]{1,0:T(8,128)(2,1)S(1)}, u32[]{:S(2)}, u32[]{:S(2)}) collective-permute-start(bf16[8,1024]{1,0:T(8,128)(2,1)S(1)} %collective-permute-done.9), channel_id=1, source_target_pairs={{0,1},{1,2},{2,3},{3,4},{4,5},{5,6},{6,7},{7,8},{8,9},{9,10},{10,1... | collective-permute-start | bytes 49160 | tf_op jit(solution)/shard_map/ppermute | solution.py:78
  266.5 5.9 %collective-permute-start.11 = (bf16[8,1024]{1,0:T(8,128)(2,1)S(1)}, bf16[8,1024]{1,0:T(8,128)(2,1)S(1)}, u32[]{:S(2)}, u32[]{:S(2)}) collective-permute-start(bf16[8,1024]{1,0:T(8,128)(2,1)S(1)} %collective-permute-done.10), channel_id=1, source_target_pairs={{0,1},{1,2},{2,3},{3,4},{4,5},{5,6},{6,7},{7,8},{8,9},{9,10},{10,1... | collective-permute-start | bytes 49160 | tf_op jit(solution)/shard_map/ppermute | solution.py:78
  272.3 5.9 %collective-permute-start.12 = (bf16[8,1024]{1,0:T(8,128)(2,1)S(1)}, bf16[8,1024]{1,0:T(8,128)(2,1)S(1)}, u32[]{:S(2)}, u32[]{:S(2)}) collective-permute-start(bf16[8,1024]{1,0:T(8,128)(2,1)S(1)} %collective-permute-done.11), channel_id=1, source_target_pairs={{0,1},{1,2},{2,3},{3,4},{4,5},{5,6},{6,7},{7,8},{8,9},{9,10},{10,1... | collective-permute-start | bytes 49160 | tf_op jit(solution)/shard_map/ppermute | solution.py:78
  278.2 5.9 %collective-permute-start.13 = (bf16[8,1024]{1,0:T(8,128)(2,1)S(1)}, bf16[8,1024]{1,0:T(8,128)(2,1)S(1)}, u32[]{:S(2)}, u32[]{:S(2)}) collective-permute-start(bf16[8,1024]{1,0:T(8,128)(2,1)S(1)} %collective-permute-done.12), channel_id=1, source_target_pairs={{0,1},{1,2},{2,3},{3,4},{4,5},{5,6},{6,7},{7,8},{8,9},{9,10},{10,1... | collective-permute-start | bytes 49160 | tf_op jit(solution)/shard_map/ppermute | solution.py:78
  284.0 5.9 %collective-permute-start.14 = (bf16[8,1024]{1,0:T(8,128)(2,1)S(1)}, bf16[8,1024]{1,0:T(8,128)(2,1)S(1)}, u32[]{:S(2)}, u32[]{:S(2)}) collective-permute-start(bf16[8,1024]{1,0:T(8,128)(2,1)S(1)} %collective-permute-done.13), channel_id=1, source_target_pairs={{0,1},{1,2},{2,3},{3,4},{4,5},{5,6},{6,7},{7,8},{8,9},{9,10},{10,1... | collective-permute-start | bytes 49160 | tf_op jit(solution)/shard_map/ppermute | solution.py:78
Sparse Core Ops, SparseCore 0:
  9.5 47.6 all-gather.1
  180.6 7.2 reduce-scatter.7
  201.2 40.7 reduce-scatter.3
  290.2 56.7 reduce-scatter.5
